TPU v7x, 32 devices: a whole 2x2x4 slice. The times are simulated.
32 devices in a mesh: members: 2 (over x), zonal: 8 (over z, y), merid: 2 (over core).
Axes of the slice: x: 2, y: 2, z: 4, core: 2. Of those that a mesh axis runs over, the one named last changes fastest.
Arguments:
- height: float32 [256, 1024], P(('members', 'zonal'), 'merid'), parts along dimension 0, may hold values from -6 to 6
- transport_u: float32 [256, 1024], P(('members', 'zonal'), 'merid'), parts along dimension 0, may hold values from -4 to 4
- transport_v: float32 [256, 1024], P(('members', 'zonal'), 'merid'), parts along dimension 0, may hold values from -4 to 4
- thickness: float32 [14, 256, 1024], P(None, ('members', 'zonal'), 'merid'), parts along dimension 1, may hold values from 0.5 to 2
- velocity_u: float32 [14, 256, 1024], P(None, ('members', 'zonal'), 'merid'), parts along dimension 1, may hold values from -3 to 3
- velocity_v: float32 [14, 256, 1024], P(None, ('members', 'zonal'), 'merid'), parts along dimension 1, may hold values from -3 to 3
- sea_faces: int32 [2, 128, 1024], P(None, 'zonal', 'merid'), may hold values 0 or 1
- wind_seeds: int32 [8, 2], P('members'), parts along dimension 0, may hold values from 1 to 96
- wind_scale: float32 [8], P('members'), parts along dimension 0, may hold values from 0.5 to 2
- wind_base: float32 [2, 128, 1024], P(None, 'zonal', 'merid'), may hold values from -6 to 6
Outputs:
- final_height: float32 [256, 1024], P(('members', 'zonal'), 'merid'), parts along dimension 0
- final_transport_u: float32 [256, 1024], P(('members', 'zonal'), 'merid'), parts along dimension 0
- final_transport_v: float32 [256, 1024], P(('members', 'zonal'), 'merid'), parts along dimension 0
- final_thickness: float32 [14, 256, 1024], P(None, ('members', 'zonal'), 'merid'), parts along dimension 1
- final_velocity_u: float32 [14, 256, 1024], P(None, ('members', 'zonal'), 'merid'), parts along dimension 1
- final_velocity_v: float32 [14, 256, 1024], P(None, ('members', 'zonal'), 'merid'), parts along dimension 1
There are 2 independent parts, one for each index of `members`. A program takes and returns all parts, laid end to end along the dimension named above; an argument that names none is the same for every part. Nothing has to cross between parts.
All inputs are finite; a program needn't handle non-finite values. No bound on the sum of `sea_faces` on one device may be relied on, other than what follows from the above.
Results may differ from a plain program's by a relative error of at most 0.0001.
Values sent between devices are 32-bit elements; how exact they have to be, the bound alone decides.
A program may use at most 64 MiB of HBM per device.

v0:
```python
import math

import jax
import jax.numpy as jnp
from jax import lax
from jax.sharding import PartitionSpec as P

NSUB = 6
STEPS = 2


WAVE_LIMIT = 0.225
STRESS_SCALE = 0.1
FLUX_STEP = 0.05
PRESS_COEF = 0.05


def extended(value, sides, width):
    for axis, dim in sides:
        devices, length = (lax.axis_size(axis), value.shape[dim])
        up = [(i, (i + 1) % devices) for i in range(devices)]
        down = [(j, i) for i, j in up]
        last = lax.slice_in_dim(value, length - width, length, axis=dim)
        leading = lax.slice_in_dim(value, 0, width, axis=dim)
        before = lax.ppermute(last, axis, up)
        after = lax.ppermute(leading, axis, down)
        value = jnp.concatenate([before, value, after], axis=dim)
    return value


def perturb(columns, rows_idx, wind_seeds, wind_scale, total_x, total_y):
    wave_x = wind_seeds[:, 0]
    wave_y = wind_seeds[:, 1]
    phase = (wave_x[:, None, None] * columns[None, :, None] % total_x).astype(jnp.float32) / total_x
    phase = (
        phase
        + (wave_y[:, None, None] * rows_idx[None, None, :] % total_y).astype(jnp.float32) / total_y
    )
    angle = 2.0 * math.pi * phase
    amplitude = wind_scale[:, None, None]
    return (
        jnp.sum(amplitude * jnp.cos(angle), axis=0),
        jnp.sum(amplitude * jnp.sin(angle), axis=0),
    )


def mirror_layers(top_rows):
    zonal_cells = top_rows.shape[1]
    whole = lax.all_gather(top_rows, "zonal", axis=1, tiled=True)
    start = (lax.axis_size("zonal") - 1 - lax.axis_index("zonal")) * zonal_cells
    piece = lax.dynamic_slice_in_dim(whole, start, zonal_cells, 1)
    return jnp.flip(piece, 1)


def mirror_static(block):
    width = block.shape[1]
    whole = lax.all_gather(block, "zonal", axis=1, tiled=True)
    start = (lax.axis_size("zonal") - 1 - lax.axis_index("zonal")) * width
    piece = lax.dynamic_slice_in_dim(whole, start, width, 1)
    return piece


def mirror_state(block):
    width = block.shape[1]
    whole = lax.all_gather(block, "zonal", axis=1, tiled=True)
    start = (lax.axis_size("zonal") - 1 - lax.axis_index("zonal")) * width
    piece = lax.dynamic_slice_in_dim(whole, start, width, 1)
    return piece


def clear_south(padded, bottom):
    first = lax.broadcasted_iota(jnp.int32, (1, 1, padded.shape[2]), 2) == 0
    return jnp.where(jnp.logical_and(bottom, first), jnp.float32(0.0), padded)


def clear_below(padded, merid_cells, margin):
    rows_ext = (
        lax.axis_index("merid") * merid_cells
        - margin
        + lax.broadcasted_iota(jnp.int32, (1, 1, padded.shape[2]), 2)
    )
    return jnp.where(rows_ext < 0, jnp.float32(0.0), padded)


def put_fold(north_field, folded, top):
    merid_cells = north_field.shape[-1]
    last = (
        lax.broadcasted_iota(jnp.int32, north_field.shape, north_field.ndim - 1) == merid_cells - 1
    )
    return jnp.where(jnp.logical_and(top, last), folded[..., None], north_field)


def from_low(field, axis):
    length = field.shape[axis]
    zero = jnp.zeros_like(lax.slice_in_dim(field, 0, 1, axis=axis))
    return jnp.concatenate([zero, lax.slice_in_dim(field, 0, length - 1, axis=axis)], axis=axis)


def from_high(field, axis):
    length = field.shape[axis]
    zero = jnp.zeros_like(lax.slice_in_dim(field, 0, 1, axis=axis))
    return jnp.concatenate([lax.slice_in_dim(field, 1, length, axis=axis), zero], axis=axis)


def advance_height(state):
    surface, flow_u, flow_v = state
    return surface - (flow_u - from_low(flow_u, 0) + flow_v - from_low(flow_v, 1))


def update_flows(surface, north_surf, state, statics):
    mask_u, mask_v, wave, stress_x, stress_y = statics
    flow_u = mask_u * (state[1] - wave * (from_high(surface, 0) - surface) + stress_x)
    flow_v = mask_v * (state[2] - wave * (north_surf - surface) + stress_y)
    return (surface, flow_u, flow_v)


def prepare_wide(mask_u, mask_v, wave, wind_base, wind_seeds, wind_scale, total_x, total_y):
    zonal_cells, merid_cells = wave.shape
    margin = NSUB + 1
    packed = jnp.stack([mask_u, mask_v, wave, wind_base[0], wind_base[1]])
    padded = extended(packed, (("zonal", 1), ("merid", 2)), margin)
    padded = clear_below(padded, merid_cells, margin)
    far = mirror_static(padded[:, :, merid_cells : merid_cells + margin])
    width = zonal_cells + 2 * margin
    spots = jnp.arange(width, dtype=jnp.int32)
    cols_own = (lax.axis_index("zonal") * zonal_cells - margin + spots) % total_x
    cols_far = (
        (lax.axis_size("zonal") - 1 - lax.axis_index("zonal")) * zonal_cells - margin + spots
    ) % total_x
    rows_own = (
        lax.axis_index("merid") * merid_cells
        - margin
        + jnp.arange(merid_cells + 2 * margin, dtype=jnp.int32)
    )
    rows_far = total_y - margin + jnp.arange(margin, dtype=jnp.int32)
    own_cos, own_sin = perturb(cols_own, rows_own, wind_seeds, wind_scale, total_x, total_y)
    far_cos, far_sin = perturb(cols_far, rows_far, wind_seeds, wind_scale, total_x, total_y)
    own = (
        padded[0],
        padded[1],
        padded[2],
        STRESS_SCALE * (padded[3] + own_cos),
        STRESS_SCALE * (padded[4] + own_sin),
    )
    mirrored = (
        far[0],
        far[1],
        far[2],
        STRESS_SCALE * (far[3] + far_cos),
        STRESS_SCALE * (far[4] + far_sin),
    )
    return (own, mirrored)


def interior(field, margin, zonal_cells, merid_cells):
    return field[margin : margin + zonal_cells, margin : margin + merid_cells]


def wide_substeps(surface, flow_u, flow_v, own, mirrored, top):
    zonal_cells, merid_cells = surface.shape
    margin = NSUB + 1
    packed = jnp.stack([surface, flow_u, flow_v])
    padded = extended(packed, (("zonal", 1), ("merid", 2)), margin)
    padded = clear_below(padded, merid_cells, margin)
    far = mirror_state(padded[:, :, merid_cells : merid_cells + margin])
    top_row = margin + merid_cells - 1
    row_ids = lax.broadcasted_iota(jnp.int32, padded.shape[1:], 1)
    fold_here = jnp.logical_and(top, row_ids == top_row)
    far_top = lax.broadcasted_iota(jnp.int32, far.shape[1:], 1) == margin - 1
    own_state = (padded[0], padded[1], padded[2])
    far_state = (far[0], far[1], far[2])
    sum_u = jnp.zeros_like(padded[1])
    sum_v = jnp.zeros_like(padded[2])
    for inner in range(NSUB):
        own_eta = advance_height(own_state)
        far_eta = advance_height(far_state)
        own_north = jnp.where(
            fold_here, jnp.flip(far_eta[:, margin - 1], 0)[:, None], from_high(own_eta, 1)
        )
        far_north = jnp.where(
            far_top, jnp.flip(own_eta[:, top_row], 0)[:, None], from_high(far_eta, 1)
        )
        own_state = update_flows(own_eta, own_north, own_state, own)
        far_state = update_flows(far_eta, far_north, far_state, mirrored)
        sum_u = sum_u + own_state[1]
        sum_v = sum_v + own_state[2]
    surface = interior(own_state[0], margin, zonal_cells, merid_cells)
    flow_u = interior(own_state[1], margin, zonal_cells, merid_cells)
    flow_v = interior(own_state[2], margin, zonal_cells, merid_cells)
    mean_u = interior(sum_u, margin, zonal_cells, merid_cells) / NSUB
    mean_v = interior(sum_v, margin, zonal_cells, merid_cells) / NSUB
    return (surface, flow_u, flow_v, mean_u, mean_v)


def layer_neighbours(thick, speed_u, speed_v, bottom, top):
    layers, zonal_cells, merid_cells = thick.shape
    folded = mirror_layers(thick[:, :, merid_cells - 1])
    packed = jnp.concatenate([thick, speed_u, speed_v], axis=0)
    padded = extended(packed, (("zonal", 1), ("merid", 2)), 1)
    padded = clear_south(padded, bottom)
    thick_pad = padded[:layers]
    west_u = padded[layers : 2 * layers, :zonal_cells, 1 : merid_cells + 1]
    south_v = padded[2 * layers :, 1 : zonal_cells + 1, :merid_cells]
    east_h = thick_pad[:, 2:, 1 : merid_cells + 1]
    west_h = thick_pad[:, :zonal_cells, 1 : merid_cells + 1]
    south_h = thick_pad[:, 1 : zonal_cells + 1, :merid_cells]
    north_h = put_fold(thick_pad[:, 1 : zonal_cells + 1, 2:], folded, top)
    return (east_h, west_h, south_h, north_h, west_u, south_v)


def body(
    height,
    transport_u,
    transport_v,
    thickness,
    velocity_u,
    velocity_v,
    sea_faces,
    wind_seeds,
    wind_scale,
    wind_base,
):
    zonal_cells, merid_cells = height.shape
    total_x = zonal_cells * lax.axis_size("zonal")
    total_y = merid_cells * lax.axis_size("merid")
    bottom = lax.axis_index("merid") == 0
    top = lax.axis_index("merid") == lax.axis_size("merid") - 1
    mask_u = sea_faces[0].astype(jnp.float32)
    mask_v = sea_faces[1].astype(jnp.float32)
    layers = thickness.shape[0]
    wave = WAVE_LIMIT / layers * jnp.sum(thickness, axis=0)
    own_static, far_static = prepare_wide(
        mask_u, mask_v, wave, wind_base, wind_seeds, wind_scale, total_x, total_y
    )
    surface, flow_u, flow_v = (height, transport_u, transport_v)
    thick, speed_u, speed_v = (thickness, velocity_u, velocity_v)
    depth_u = None
    depth_v = None
    for outer in range(STEPS):
        east_h, west_h, south_h, north_h, west_u, south_v = layer_neighbours(
            thick, speed_u, speed_v, bottom, top
        )
        thick_u = (thick + east_h) * 0.5
        thick_v = (thick + north_h) * 0.5
        if depth_u is None:
            depth_u = jnp.sum(thick_u, axis=0)
            depth_v = jnp.sum(thick_v, axis=0)
        surface, flow_u, flow_v, mean_u, mean_v = wide_substeps(
            surface, flow_u, flow_v, own_static, far_static, top
        )
        flux_u = speed_u * thick_u
        flux_v = speed_v * thick_v
        west_flux = west_u * (west_h + thick) * 0.5
        south_flux = south_v * (south_h + thick) * 0.5
        pressure = jnp.cumsum(thick, axis=0)
        east_press = jnp.cumsum(east_h, axis=0)
        north_press = jnp.cumsum(north_h, axis=0)
        trial_u = speed_u - PRESS_COEF * (east_press - pressure)
        trial_v = speed_v - PRESS_COEF * (north_press - pressure)
        speed_u = mask_u * (trial_u + (mean_u - jnp.sum(thick_u * trial_u, axis=0)) / depth_u)
        speed_v = mask_v * (trial_v + (mean_v - jnp.sum(thick_v * trial_v, axis=0)) / depth_v)
        thick = thick - FLUX_STEP * (flux_u - west_flux + flux_v - south_flux)
    return (surface, flow_u, flow_v, thick, speed_u, speed_v)


def solution(mesh):
    placed = (
        P(("members", "zonal"), "merid"),
        P(("members", "zonal"), "merid"),
        P(("members", "zonal"), "merid"),
        P(None, ("members", "zonal"), "merid"),
        P(None, ("members", "zonal"), "merid"),
        P(None, ("members", "zonal"), "merid"),
        P(None, "zonal", "merid"),
        P("members", None),
        P("members"),
        P(None, "zonal", "merid"),
    )
    return jax.shard_map(
        body,
        mesh=mesh,
        in_specs=placed,
        out_specs=(
            P(("members", "zonal"), "merid"),
            P(("members", "zonal"), "merid"),
            P(("members", "zonal"), "merid"),
            P(None, ("members", "zonal"), "merid"),
            P(None, ("members", "zonal"), "merid"),
            P(None, ("members", "zonal"), "merid"),
        ),
        check_vma=False,
    )
```

profile of v0, /device:TPU:0, one launch (start us, length us, event | category | flops | bytes accessed | tf_op | source)
XLA Modules:
  0.0 285.9 jit_solution(3082873381220074941)
XLA Ops:
  4.0 3.0 %collective-permute-start.12 = (f32[42,1,512]{2,1,0:T(1,128)S(1)}, f32[42,1,512]{2,1,0:T(1,128)}, u32[]{:S(2)}, u32[]{:S(2)}) collective-permute-start(f32[42,1,512]{2,1,0:T(1,128)S(1)} %get-tuple-element.64), channel_id=1, source_target_pairs={{0,2},{2,4},{4,6},{6,8},{8,10},{10,12},{12,14},{14,0},{1,3},{3,5},... | collective-permute-start | bytes 258056 | tf_op jit(solution)/shard_map/ppermute | solution.py:25
  7.0 3.0 %collective-permute-start.13 = (f32[42,1,512]{2,1,0:T(1,128)}, f32[42,1,512]{2,1,0:T(1,128)}, u32[]{:S(2)}, u32[]{:S(2)}) collective-permute-start(f32[42,1,512]{2,1,0:T(1,128)} %get-tuple-element.63), channel_id=1, source_target_pairs={{2,0},{4,2},{6,4},{8,6},{10,8},{12,10},{14,12},{0,14},{3,1},{5,3},... | collective-permute-start | bytes 258056 | tf_op jit(solution)/shard_map/ppermute | solution.py:26
  10.1 4.7 %collective-permute-start.1 = (f32[3,7,512]{2,1,0:T(8,128)S(1)}, f32[3,7,512]{2,1,0:T(8,128)S(1)}, u32[]{:S(2)}, u32[]{:S(2)}) collective-permute-start(f32[3,7,512]{2,1,0:T(8,128)S(1)} %get-tuple-element.111), channel_id=1, source_target_pairs={{2,0},{4,2},{6,4},{8,6},{10,8},{12,10},{14,12},{0,14},{3,1},{5,3},... | collective-permute-start | bytes 129032 | tf_op jit(solution)/shard_map/ppermute | solution.py:26
  14.9 2.2 fusion.143
  18.0 30.5 %all-gather = f32[14,128,1]{0,2,1:T(1,128)S(1)} all-gather(f32[14,16,1]{0,2,1:T(1,128)S(1)} %copy.262), channel_id=2, replica_groups=mesh['members'=2,'zonal'=8,'merid'=2] {'zonal'}, dimensions={1}, use_global_device_ids=true | all-gather | bytes 8064 | tf_op jit(solution)/shard_map/all_gather | solution.py:49
  50.4 3.6 %multiply_reduce_fusion.5 = (f32[30,526]{1,0:T(8,128)}, f32[30,526]{1,0:T(8,128)}) fusion(f32[4,526]{1,0:T(4,128)S(1)} %fusion.56, f32[4,30]{0,1:T(8,128)S(1)} %copy.207, f32[4]{0:T(128)S(1)} %copy-done.60), kind=kLoop, calls=%fused_computation.59 | loop fusion | flops 347160 | bytes 135152 | tf_op jit(solution)/shard_map/reduce_sum | solution.py:42
  55.9 31.3 %all_gather.15 = f32[3,240,7]{2,0,1:T(4,128)S(1)} all-gather(f32[3,30,7]{2,0,1:T(4,128)S(1)} %copy.208), channel_id=1, replica_groups=mesh['members'=2,'zonal'=8,'merid'=2] {'zonal'}, dimensions={1}, use_global_device_ids=true | all-gather | bytes 22680 | tf_op jit(solution)/shard_map/all_gather | solution.py:65
  94.3 1.9 pad_maximum_fusion
  98.1 2.9 %multiply_reduce_fusion.3 = (f32[16,512]{1,0:T(8,128)}, f32[16,512]{1,0:T(8,128)}, f32[16,512]{1,0:T(8,128)S(1)}, f32[16,512]{1,0:T(8,128)}, f32[16,512]{1,0:T(8...) fusion(f32[14,16,512]{2,1,0:T(8,128)S(1)} %copy-done, f32[42,18,514]{2,1,0:T(8,128)S(1)} %copy_select_fusion.1, ...), kind=kOutput, calls=%fused_computation.52 | output fusion | flops 4661248 | bytes 6595072 | tf_op jit(solution)/shard_map/jit(cumsum)/reduce_window_sum | solution.py:256
  101.1 4.7 %collective-permute-start.5 = (f32[5,7,512]{2,1,0:T(8,128)S(1)}, f32[5,7,512]{2,1,0:T(8,128)S(1)}, u32[]{:S(2)}, u32[]{:S(2)}) collective-permute-start(f32[5,7,512]{2,1,0:T(8,128)S(1)} %get-tuple-element.107), channel_id=1, source_target_pairs={{2,0},{4,2},{6,4},{8,6},{10,8},{12,10},{14,12},{0,14},{3,1},{5,3},... | collective-permute-start | bytes 215048 | tf_op jit(solution)/shard_map/ppermute | solution.py:26
  105.8 2.2 fusion.144
  108.4 30.5 %all-gather.1 = f32[14,128,1]{0,2,1:T(1,128)S(1)} all-gather(f32[14,16,1]{0,2,1:T(1,128)S(1)} %copy.232), channel_id=3, replica_groups=mesh['members'=2,'zonal'=8,'merid'=2] {'zonal'}, dimensions={1}, use_global_device_ids=true | all-gather | bytes 8064 | tf_op jit(solution)/shard_map/all_gather | solution.py:49
  140.8 32.8 %all_gather.16 = f32[5,240,7]{2,0,1:T(8,128)S(1)} all-gather(f32[5,30,7]{2,0,1:T(8,128)S(1)} %copy.210), channel_id=1, replica_groups=mesh['members'=2,'zonal'=8,'merid'=2] {'zonal'}, dimensions={1}, use_global_device_ids=true | all-gather | bytes 37800 | tf_op jit(solution)/shard_map/all_gather | solution.py:57
  185.1 4.7 %collective-permute-start.9 = (f32[3,7,512]{2,1,0:T(8,128)S(1)}, f32[3,7,512]{2,1,0:T(8,128)S(1)}, u32[]{:S(2)}, u32[]{:S(2)}) collective-permute-start(f32[3,7,512]{2,1,0:T(8,128)S(1)} %get-tuple-element.109), channel_id=1, source_target_pairs={{2,0},{4,2},{6,4},{8,6},{10,8},{12,10},{14,12},{0,14},{3,1},{5,3},... | collective-permute-start | bytes 129032 | tf_op jit(solution)/shard_map/ppermute | solution.py:26
  193.4 4.7 %collective-permute-start.17 = (f32[42,1,512]{2,1,0:T(1,128)}, f32[42,1,512]{2,1,0:T(1,128)}, u32[]{:S(2)}, u32[]{:S(2)}) collective-permute-start(f32[42,1,512]{2,1,0:T(1,128)} %get-tuple-element.61), channel_id=1, source_target_pairs={{2,0},{4,2},{6,4},{8,6},{10,8},{12,10},{14,12},{0,14},{3,1},{5,3},... | collective-permute-start | bytes 258056 | tf_op jit(solution)/shard_map/ppermute | solution.py:26
  199.8 31.5 %all_gather.17 = f32[3,240,7]{2,0,1:T(4,128)S(1)} all-gather(f32[3,30,7]{2,0,1:T(4,128)S(1)} %copy.212), channel_id=1, replica_groups=mesh['members'=2,'zonal'=8,'merid'=2] {'zonal'}, dimensions={1}, use_global_device_ids=true | all-gather | bytes 22680 | tf_op jit(solution)/shard_map/all_gather | solution.py:65
  239.7 1.4 rev.85
  246.5 1.4 rev.87
  258.8 1.3 slice_bitcast_fusion.18
  261.4 1.3 rev.91
  266.0 1.3 rev.93
  279.3 1.6 multiply_reduce_fusion
  280.9 1.7 fusion.46
  283.4 1.7 fusion.42
  (377 shorter events, 78.4 us)
Async XLA Ops:
  4.0 83.5 %collective-permute-start.12 = (f32[42,1,512]{2,1,0:T(1,128)S(1)}, f32[42,1,512]{2,1,0:T(1,128)}, u32[]{:S(2)}, u32[]{:S(2)}) collective-permute-start(f32[42,1,512]{2,1,0:T(1,128)S(1)} %get-tuple-element.64), channel_id=1, source_target_pairs={{0,2},{2,4},{4,6},{6,8},{8,10},{10,12},{12,14},{14,0},{1,3},{3,5},... | collective-permute-start | bytes 258056 | tf_op jit(solution)/shard_map/ppermute | solution.py:25
  7.0 82.2 %collective-permute-start.13 = (f32[42,1,512]{2,1,0:T(1,128)}, f32[42,1,512]{2,1,0:T(1,128)}, u32[]{:S(2)}, u32[]{:S(2)}) collective-permute-start(f32[42,1,512]{2,1,0:T(1,128)} %get-tuple-element.63), channel_id=1, source_target_pairs={{2,0},{4,2},{6,4},{8,6},{10,8},{12,10},{14,12},{0,14},{3,1},{5,3},... | collective-permute-start | bytes 258056 | tf_op jit(solution)/shard_map/ppermute | solution.py:26
  10.0 44.0 %collective-permute-start = (f32[3,7,512]{2,1,0:T(8,128)S(1)}, f32[3,7,512]{2,1,0:T(8,128)S(1)}, u32[]{:S(2)}, u32[]{:S(2)}) collective-permute-start(f32[3,7,512]{2,1,0:T(8,128)S(1)} %get-tuple-element.110), channel_id=1, source_target_pairs={{0,2},{2,4},{4,6},{6,8},{8,10},{10,12},{12,14},{14,0},{1,3},{3,5},... | collective-permute-start | bytes 129032 | tf_op jit(solution)/shard_map/ppermute | solution.py:25
  10.1 43.9 %collective-permute-start.1 = (f32[3,7,512]{2,1,0:T(8,128)S(1)}, f32[3,7,512]{2,1,0:T(8,128)S(1)}, u32[]{:S(2)}, u32[]{:S(2)}) collective-permute-start(f32[3,7,512]{2,1,0:T(8,128)S(1)} %get-tuple-element.111), channel_id=1, source_target_pairs={{2,0},{4,2},{6,4},{8,6},{10,8},{12,10},{14,12},{0,14},{3,1},{5,3},... | collective-permute-start | bytes 129032 | tf_op jit(solution)/shard_map/ppermute | solution.py:26
  17.2 70.2 %copy-start.51 = (pred[526]{0:T(1024)(128)(4,1)}, pred[526]{0:T(1024)(128)(4,1)S(1)}, u32[]{:S(2)}) copy-start(pred[526]{0:T(1024)(128)(4,1)S(1)} %broadcast_compare_fusion) | copy-start | bytes 1582
  54.1 1.3 collective-permute-start.2
  54.2 1.4 collective-permute-start.3
  91.1 3.3 %collective-permute-start.14 = (f32[42,18,1]{2,0,1:T(8,128)}, f32[42,18,1]{2,0,1:T(8,128)}, u32[]{:S(2)}, u32[]{:S(2)}) collective-permute-start(f32[42,18,1]{2,0,1:T(8,128)} %get-tuple-element.59), channel_id=1, source_target_pairs={{0,1},{1,0},{2,3},{3,2},{4,5},{5,4},{6,7},{7,6},{8,9},{9,8},{10,11... | collective-permute-start | bytes 9080 | tf_op jit(solution)/shard_map/ppermute | solution.py:25
  91.1 3.3 %collective-permute-start.15 = (f32[42,18,1]{2,0,1:T(8,128)}, f32[42,18,1]{2,0,1:T(8,128)}, u32[]{:S(2)}, u32[]{:S(2)}) collective-permute-start(f32[42,18,1]{2,0,1:T(8,128)} %get-tuple-element.60), channel_id=1, source_target_pairs={{1,0},{0,1},{3,2},{2,3},{5,4},{4,5},{7,6},{6,7},{9,8},{8,9},{11,10... | collective-permute-start | bytes 9080 | tf_op jit(solution)/shard_map/ppermute | solution.py:26
  101.1 37.8 %collective-permute-start.4 = (f32[5,7,512]{2,1,0:T(8,128)S(1)}, f32[5,7,512]{2,1,0:T(8,128)S(1)}, u32[]{:S(2)}, u32[]{:S(2)}) collective-permute-start(f32[5,7,512]{2,1,0:T(8,128)S(1)} %get-tuple-element.106), channel_id=1, source_target_pairs={{0,2},{2,4},{4,6},{6,8},{8,10},{10,12},{12,14},{14,0},{1,3},{3,5},... | collective-permute-start | bytes 215048 | tf_op jit(solution)/shard_map/ppermute | solution.py:25
  101.1 37.8 %collective-permute-start.5 = (f32[5,7,512]{2,1,0:T(8,128)S(1)}, f32[5,7,512]{2,1,0:T(8,128)S(1)}, u32[]{:S(2)}, u32[]{:S(2)}) collective-permute-start(f32[5,7,512]{2,1,0:T(8,128)S(1)} %get-tuple-element.107), channel_id=1, source_target_pairs={{2,0},{4,2},{6,4},{8,6},{10,8},{12,10},{14,12},{0,14},{3,1},{5,3},... | collective-permute-start | bytes 215048 | tf_op jit(solution)/shard_map/ppermute | solution.py:26
  108.1 67.5 %copy-start.45 = (pred[7]{0:T(512)(128)(4,1)S(1)}, pred[7]{0:T(512)(128)(4,1)}, u32[]{:S(2)}) copy-start(pred[7]{0:T(512)(128)(4,1)} %iota_compare_fusion.3) | copy-start | bytes 25
  108.1 67.4 %copy-start.48 = (f32[30,7]{0,1:T(8,128)S(1)}, f32[30,7]{0,1:T(8,128)}, u32[]{:S(2)}) copy-start(f32[30,7]{0,1:T(8,128)} %get-tuple-element.41) | copy-start | bytes 2524
  108.1 67.4 %copy-start.49 = (f32[30,7]{0,1:T(8,128)S(1)}, f32[30,7]{0,1:T(8,128)}, u32[]{:S(2)}) copy-start(f32[30,7]{0,1:T(8,128)} %get-tuple-element.42) | copy-start | bytes 2524
  139.0 1.3 collective-permute-start.6
  139.1 1.4 collective-permute-start.7
  185.1 6.8 %collective-permute-start.8 = (f32[3,7,512]{2,1,0:T(8,128)S(1)}, f32[3,7,512]{2,1,0:T(8,128)S(1)}, u32[]{:S(2)}, u32[]{:S(2)}) collective-permute-start(f32[3,7,512]{2,1,0:T(8,128)S(1)} %get-tuple-element.108), channel_id=1, source_target_pairs={{0,2},{2,4},{4,6},{6,8},{8,10},{10,12},{12,14},{14,0},{1,3},{3,5},... | collective-permute-start | bytes 129032 | tf_op jit(solution)/shard_map/ppermute | solution.py:25
  185.1 6.8 %collective-permute-start.9 = (f32[3,7,512]{2,1,0:T(8,128)S(1)}, f32[3,7,512]{2,1,0:T(8,128)S(1)}, u32[]{:S(2)}, u32[]{:S(2)}) collective-permute-start(f32[3,7,512]{2,1,0:T(8,128)S(1)} %get-tuple-element.109), channel_id=1, source_target_pairs={{2,0},{4,2},{6,4},{8,6},{10,8},{12,10},{14,12},{0,14},{3,1},{5,3},... | collective-permute-start | bytes 129032 | tf_op jit(solution)/shard_map/ppermute | solution.py:26
  192.0 6.1 %collective-permute-start.10 = (f32[3,30,7]{2,1,0:T(8,128)S(1)}, f32[3,30,7]{2,1,0:T(8,128)S(1)}, u32[]{:S(2)}, u32[]{:S(2)}) collective-permute-start(f32[3,30,7]{2,1,0:T(8,128)S(1)} %get-tuple-element.102), channel_id=1, source_target_pairs={{0,1},{1,0},{2,3},{3,2},{4,5},{5,4},{6,7},{7,6},{8,9},{9,8},{10,11... | collective-permute-start | bytes 7568 | tf_op jit(solution)/shard_map/ppermute | solution.py:25
  192.1 6.0 %collective-permute-start.11 = (f32[3,30,7]{2,1,0:T(8,128)S(1)}, f32[3,30,7]{2,1,0:T(8,128)S(1)}, u32[]{:S(2)}, u32[]{:S(2)}) collective-permute-start(f32[3,30,7]{2,1,0:T(8,128)S(1)} %get-tuple-element.103), channel_id=1, source_target_pairs={{1,0},{0,1},{3,2},{2,3},{5,4},{4,5},{7,6},{6,7},{9,8},{8,9},{11,10... | collective-permute-start | bytes 7568 | tf_op jit(solution)/shard_map/ppermute | solution.py:26
  193.4 78.0 %collective-permute-start.16 = (f32[42,1,512]{2,1,0:T(1,128)}, f32[42,1,512]{2,1,0:T(1,128)}, u32[]{:S(2)}, u32[]{:S(2)}) collective-permute-start(f32[42,1,512]{2,1,0:T(1,128)} %get-tuple-element.62), channel_id=1, source_target_pairs={{0,2},{2,4},{4,6},{6,8},{8,10},{10,12},{12,14},{14,0},{1,3},{3,5},... | collective-permute-start | bytes 258056 | tf_op jit(solution)/shard_map/ppermute | solution.py:25
  193.4 79.7 %collective-permute-start.17 = (f32[42,1,512]{2,1,0:T(1,128)}, f32[42,1,512]{2,1,0:T(1,128)}, u32[]{:S(2)}, u32[]{:S(2)}) collective-permute-start(f32[42,1,512]{2,1,0:T(1,128)} %get-tuple-element.61), channel_id=1, source_target_pairs={{2,0},{4,2},{6,4},{8,6},{10,8},{12,10},{14,12},{0,14},{3,1},{5,3},... | collective-permute-start | bytes 258056 | tf_op jit(solution)/shard_map/ppermute | solution.py:26
  274.2 1.9 collective-permute-start.18
  274.3 2.4 collective-permute-start.19
  (57 other events, 646.5 us)
where the time goes:
time: 288 us; the launch traced here: 286 us
  blocking collectives  157 us (55%)
  local copies, waits for them, and re-layouts  52 us (18%)
  other arithmetic  46 us (16%)
  starting transfers between devices  27.8 us (10%)
    all_gather x2, blocking collectives, mirror_state(): whole = lax.all_gather(block, 'zonal', axis=1, tiled=True)  62.7 us
    all_gather x2, blocking collectives, mirror_layers(): whole = lax.all_gather(top_rows, 'zonal', axis=1, tiled=True)  61 us
    all_gather x1, blocking collectives, mirror_static(): whole = lax.all_gather(block, 'zonal', axis=1, tiled=True)  32.8 us
    ppermute x10, starting transfers between devices, extended(): after = lax.ppermute(leading, axis, down)  24.4 us
    slice x44, local copies, waits for them, and re-layouts, from_high(): lax.slice_in_dim(field, 1, length, axis=axis)  15.4 us
    unnamed x144, local copies, waits for them, and re-layouts  12.2 us
    mul x21, other arithmetic, update_flows(): mask_u * (state[1] - wave * (from_high(surface, 0) - surface) + stress_x)  12.1 us
    rev x12, local copies, waits for them, and re-layouts, wide_substeps(): jnp.flip(far_eta[:, margin - 1], 0)[:, None]  6.69 us
  transfers between devices with their start and end apart: 20, of which 6 were waited for; matrix products, arithmetic and copies ran while one was open for 21% of the time, Pallas kernels for 0%

commit v1 on v0

v1 whole, which is shorter than its diff:
```python
import functools
import math

import jax
import jax.numpy as jnp
from jax import lax
from jax.experimental import pallas as pl
from jax.experimental.pallas import tpu as pltpu
from jax.sharding import PartitionSpec as P

NSUB = 6
STEPS = 2
MARGIN = NSUB * STEPS

WAVE_LIMIT = 0.225
STRESS_SCALE = 0.1
FLUX_STEP = 0.05
PRESS_COEF = 0.05
LANES = 128
FIELDS = 8
SLOT = LANES // FIELDS
MESH = pl.DeviceIdType.MESH


def roll(value, shift, axis):
    return pltpu.roll(value, shift % value.shape[axis], axis)


def iota(shape, axis):
    return lax.broadcasted_iota(jnp.int32, shape, axis)


def turns(seed, index, total):
    part = seed * index * (1.0 / total)
    angle = (2.0 * math.pi) * (part - jnp.floor(part))
    return jnp.cos(angle), jnp.sin(angle)


def kernel(
    zonal_devices,
    merid_devices,
    height,
    trans_u,
    trans_v,
    thick,
    vel_u,
    vel_v,
    faces,
    seeds,
    scale,
    base,
    o_eta,
    o_bu,
    o_bv,
    o_h,
    o_u,
    o_v,
    X,
    G,
    wind_own,
    wind_far,
    half_send,
    half_recv,
    pack_send,
    inner_recv,
    fold_recv,
    mean,
    depth,
    lay_send_r,
    lay_send_l,
    lay_recv_w,
    lay_recv_e,
    lay_pack_send,
    lay_pack_recv,
    send_sem,
    recv_sem,
    lay_send_sem,
    lay_recv_sem,
):
    layers, nx, ny = thick.shape
    Z = zonal_devices
    total_x, total_y = nx * Z, ny * merid_devices
    z = lax.axis_index("zonal")
    m = lax.axis_index("merid")
    other = 1 - m
    bottom = m == 0
    top = m == merid_devices - 1
    right, left = lax.rem(z + 1, Z), lax.rem(z + Z - 1, Z)
    mirror = Z - 1 - z
    mirror_e, mirror_w = lax.rem(mirror + 1, Z), lax.rem(mirror + Z - 1, Z)
    extra = MARGIN - 8
    rows = 3 * nx
    width = ny + LANES
    last = ny - LANES

    barrier = pltpu.get_barrier_semaphore()
    for zz, mm in ((left, m), (right, m), (left, other), (right, other), (z, other)):
        pl.semaphore_signal(barrier, inc=1, device_id={"zonal": zz, "merid": mm}, device_id_type=MESH)
    for zz in (mirror_w, mirror, mirror_e):

        @pl.when(jnp.logical_and(top, zz != z))
        def _():
            pl.semaphore_signal(barrier, inc=1, device_id={"zonal": zz}, device_id_type=MESH)

    own = slice(nx, 2 * nx)
    X[0, own, 0:ny] = height[...]
    X[1, own, 0:ny] = trans_u[...]
    X[2, own, 0:ny] = trans_v[...]
    X[3, own, 0:ny] = faces[0].astype(jnp.float32)
    X[4, own, 0:ny] = faces[1].astype(jnp.float32)
    total = thick[0]
    for l in range(1, layers):
        total = total + thick[l]
    X[5, own, 0:ny] = (WAVE_LIMIT / layers) * total
    X[6, own, 0:ny] = base[0]
    X[7, own, 0:ny] = base[1]
    for f in range(FIELDS):
        half_send[0, f * extra : (f + 1) * extra, :] = X[f, 2 * nx - MARGIN : 2 * nx - 8, 0:ny]
        half_send[1, f * extra : (f + 1) * extra, :] = X[f, nx + 8 : nx + MARGIN, 0:ny]
    lane = iota((nx, LANES), 1)
    inner = jnp.zeros((nx, LANES), jnp.float32)
    crest = jnp.zeros((nx, LANES), jnp.float32)
    for f in range(FIELDS):
        here = jnp.logical_and(lane >= f * SLOT, lane < (f + 1) * SLOT)
        high = roll(X[f, own, last:ny], SLOT * (f + 1), 1)
        low = roll(X[f, own, 0:LANES], SLOT * f, 1)
        crest = jnp.where(here, high, crest)
        inner = jnp.where(here, jnp.where(bottom, high, low), inner)
    pack_send[0] = inner
    pack_send[2] = crest
    for r in range(nx):
        pack_send[1, r : r + 1, :] = pack_send[2, nx - 1 - r : nx - r, :]

    across = sum((zz != z).astype(jnp.int32) for zz in (mirror_w, mirror, mirror_e))
    pl.semaphore_wait(barrier, 5 + jnp.where(top, across, 0))

    def send(src, dst, k, zz, mm):
        return pltpu.make_async_remote_copy(
            src_ref=src,
            dst_ref=dst,
            send_sem=send_sem.at[k],
            recv_sem=recv_sem.at[k],
            device_id={"zonal": zz, "merid": mm},
            device_id_type=MESH,
        )

    copies = [
        send(X.at[:, nx : nx + 8, 0:ny], X.at[:, 2 * nx : 2 * nx + 8, 0:ny], 0, left, m),
        send(X.at[:, 2 * nx - 8 : 2 * nx, 0:ny], X.at[:, nx - 8 : nx, 0:ny], 1, right, m),
        send(half_send.at[0], half_recv.at[0], 2, right, m),
        send(half_send.at[1], half_recv.at[1], 3, left, m),
        send(pack_send.at[0], inner_recv.at[2], 4, left, other),
        send(pack_send.at[0], inner_recv.at[1], 5, z, other),
        send(pack_send.at[0], inner_recv.at[0], 6, right, other),
    ]
    folds = [
        (send(pack_send.at[1], fold_recv.at[s], 7 + s, zz, m),
         pltpu.make_async_copy(pack_send.at[1], fold_recv.at[s], recv_sem.at[7 + s]), zz)
        for s, zz in ((2, mirror_w), (1, mirror), (0, mirror_e))
    ]
    for copy in copies[4:]:
        copy.start()
    for far_copy, near_copy, zz in folds:

        @pl.when(jnp.logical_and(top, zz != z))
        def _():
            far_copy.start()

        @pl.when(jnp.logical_and(top, zz == z))
        def _():
            near_copy.start()

    for copy in copies[:4]:
        copy.start()

    def lay_copies(step):
        def one(src, dst, k, zz, mm):
            return pltpu.make_async_remote_copy(
                src_ref=src,
                dst_ref=dst,
                send_sem=lay_send_sem.at[step, k],
                recv_sem=lay_recv_sem.at[step, k],
                device_id={"zonal": zz, "merid": mm},
                device_id_type=MESH,
            )

        return [
            one(lay_send_r.at[step], lay_recv_w.at[step], 0, right, m),
            one(lay_send_l.at[step], lay_recv_e.at[step], 1, left, m),
            one(lay_pack_send.at[step, 0], lay_pack_recv.at[step, 0], 2, z, other),
            one(lay_pack_send.at[step, 1], lay_pack_recv.at[step, 1], 3, mirror, m),
        ]

    above = lay_send_r.shape[1] // 2

    def send_layers(step, h_ref, u_ref, v_ref):
        edge = jnp.zeros((nx, LANES), jnp.float32)
        brim = jnp.zeros((nx, LANES), jnp.float32)
        for l in range(layers):
            lay_send_r[step, l : l + 1, :] = h_ref[l, nx - 1 : nx, :]
            lay_send_r[step, above + l : above + l + 1, :] = u_ref[l, nx - 1 : nx, :]
            lay_send_l[step, l : l + 1, :] = h_ref[l, 0:1, :]
            high = roll(h_ref[l, :, last:ny], l + 1, 1)
            low = roll(h_ref[l, :, 0:LANES], l, 1)
            high_v = roll(v_ref[l, :, last:ny], layers + l + 1, 1)
            edge = jnp.where(lane == l, jnp.where(bottom, high, low), edge)
            edge = jnp.where(lane == layers + l, high_v, edge)
            brim = jnp.where(lane == l, high, brim)
        lay_pack_send[step, 0] = edge
        lay_pack_send[step, 2] = brim
        for r in range(nx):
            lay_pack_send[step, 1, r : r + 1, :] = lay_pack_send[step, 2, nx - 1 - r : nx - r, :]
        out = lay_copies(step)
        for copy in out[:3]:
            copy.start()

        @pl.when(top)
        def _():
            out[3].start()

        return out

    def wait_layers(out):
        for copy in out[:3]:
            copy.wait()

        @pl.when(top)
        def _():
            out[3].wait()

    out = send_layers(0, thick, vel_u, vel_v)

    first = (z * nx - nx).astype(jnp.float32)
    col = first + iota((rows, 1), 0).astype(jnp.float32) + float(total_x)
    far_col = float(2 * total_x - 1) - (first + iota((rows, 1), 0).astype(jnp.float32))
    spot = iota((1, width), 1)
    row = spot + m * ny
    row = jnp.where(jnp.logical_and(top, spot >= ny), row - width, row).astype(jnp.float32)
    far_row = (iota((1, LANES), 1) + (total_y - LANES)).astype(jnp.float32)
    px = jnp.zeros((rows, width), jnp.float32)
    py = jnp.zeros((rows, width), jnp.float32)
    fx = jnp.zeros((rows, LANES), jnp.float32)
    fy = jnp.zeros((rows, LANES), jnp.float32)
    for k in range(seeds.shape[0]):
        seed_x = seeds[k, 0].astype(jnp.float32)
        seed_y = seeds[k, 1].astype(jnp.float32)
        ca, sa = turns(seed_x, col, total_x)
        cf, sf = turns(seed_x, far_col, total_x)
        cb, sb = turns(seed_y, row, total_y)
        cg, sg = turns(seed_y, far_row, total_y)
        amp = scale[k]
        ca, sa, cf, sf = amp * ca, amp * sa, amp * cf, amp * sf
        px = px + (ca * cb - sa * sb)
        py = py + (sa * cb + ca * sb)
        fx = fx + (cf * cg - sf * sg)
        fy = fy + (sf * cg + cf * sg)
    wind_own[0] = px
    wind_own[1] = py
    wind_far[0] = fx
    wind_far[1] = fy

    for copy in copies:
        copy.wait()
    for far_copy, near_copy, zz in folds:

        @pl.when(jnp.logical_and(top, zz != z))
        def _():
            far_copy.wait()

        @pl.when(jnp.logical_and(top, zz == z))
        def _():
            near_copy.wait()

    for f in range(FIELDS):
        X[f, nx - MARGIN : nx - 8, 0:ny] = half_recv[0, f * extra : (f + 1) * extra, :]
        X[f, 2 * nx + 8 : 2 * nx + MARGIN, 0:ny] = half_recv[1, f * extra : (f + 1) * extra, :]
        for s in range(3):
            got = inner_recv[s]
            part = slice(s * nx, (s + 1) * nx)
            X[f, part, ny:width] = jnp.where(
                top, roll(got, LANES - SLOT * (f + 1), 1), roll(got, LANES - SLOT * f, 1)
            )
            G[f, part, :] = roll(fold_recv[s], LANES - SLOT * (f + 1), 1)
    for k in range(2):
        X[6 + k] = STRESS_SCALE * (X[6 + k] + wind_own[k])
        G[6 + k] = STRESS_SCALE * (G[6 + k] + wind_far[k])

    lanes = iota((rows, width), 1)
    wall = jnp.logical_and(bottom, lanes == 0)
    crown = jnp.logical_and(top, lanes == ny - 1)
    far_top = iota((rows, LANES), 1) == LANES - 1

    def substep(_, carry):
        eta, bu, bv = X[0], X[1], X[2]
        g_eta, g_bu, g_bv = G[0], G[1], G[2]
        eta = eta - (bu - roll(bu, 1, 0) + bv - jnp.where(wall, 0.0, roll(bv, 1, 1)))
        g_eta = g_eta - (g_bu - roll(g_bu, -1, 0) + g_bv - roll(g_bv, 1, 1))
        north = jnp.where(crown, g_eta[:, LANES - 1 :], roll(eta, -1, 1))
        g_north = jnp.where(far_top, eta[:, ny - 1 : ny], roll(g_eta, -1, 1))
        bu = X[3] * (bu - X[5] * (roll(eta, -1, 0) - eta) + X[6])
        bv = X[4] * (bv - X[5] * (north - eta) + X[7])
        g_bu = G[3] * (g_bu - G[5] * (roll(g_eta, 1, 0) - g_eta) + G[6])
        g_bv = G[4] * (g_bv - G[5] * (g_north - g_eta) + G[7])
        X[0], X[1], X[2] = eta, bu, bv
        G[0], G[1], G[2] = g_eta, g_bu, g_bv
        mean[0] = mean[0] + bu[nx : 2 * nx, 0:ny]
        mean[1] = mean[1] + bv[nx : 2 * nx, 0:ny]
        return carry

    def substeps():
        mean[...] = jnp.zeros_like(mean)
        lax.fori_loop(0, NSUB, substep, 0)

    row_id = iota((nx, ny), 0)
    lane_id = iota((nx, ny), 1)
    at_west = row_id == 0
    at_east = row_id == nx - 1
    at_south = lane_id == 0
    at_north = lane_id == ny - 1

    def layer_step(step, h_ref, u_ref, v_ref):
        zero = jnp.zeros((nx, ny), jnp.float32)
        press_u, press_v, sum_u, sum_v = zero, zero, zero, zero
        deep_u, deep_v = zero, zero
        for l in range(layers):
            h, u, v = h_ref[l], u_ref[l], v_ref[l]
            side = lay_pack_recv[step, 0, :, l : l + 1]
            cap = jnp.where(top, lay_pack_recv[step, 1, :, l : l + 1], side)
            south_v = lay_pack_recv[step, 0, :, layers + l : layers + l + 1]
            h_east = jnp.where(at_east, lay_recv_e[step, l : l + 1, :], roll(h, -1, 0))
            h_north = jnp.where(at_north, cap, roll(h, -1, 1))
            hu = (h + h_east) * 0.5
            hv = (h + h_north) * 0.5
            if step == 0:
                deep_u = deep_u + hu
                deep_v = deep_v + hv
            flux_u = u * hu
            flux_v = v * hv
            west_row = lay_recv_w[step, above + l : above + l + 1, :] * (
                (lay_recv_w[step, l : l + 1, :] + h[0:1, :]) * 0.5
            )
            south_col = jnp.where(top, south_v * ((side + h[:, 0:1]) * 0.5), 0.0)
            flux_w = jnp.where(at_west, west_row, roll(flux_u, 1, 0))
            flux_s = jnp.where(at_south, south_col, roll(flux_v, 1, 1))
            press_u = press_u + (h_east - h)
            press_v = press_v + (h_north - h)
            trial_u = u - PRESS_COEF * press_u
            trial_v = v - PRESS_COEF * press_v
            sum_u = sum_u + hu * trial_u
            sum_v = sum_v + hv * trial_v
            o_u[l] = trial_u
            o_v[l] = trial_v
            o_h[l] = h - FLUX_STEP * (flux_u - flux_w + flux_v - flux_s)
        if step == 0:
            depth[0] = 1.0 / deep_u
            depth[1] = 1.0 / deep_v
        fix_u = (mean[0] * (1.0 / NSUB) - sum_u) * depth[0]
        fix_v = (mean[1] * (1.0 / NSUB) - sum_v) * depth[1]
        mask_u, mask_v = X[3, own, 0:ny], X[4, own, 0:ny]
        for l in range(layers):
            o_u[l] = mask_u * (o_u[l] + fix_u)
            o_v[l] = mask_v * (o_v[l] + fix_v)

    substeps()
    wait_layers(out)
    layer_step(0, thick, vel_u, vel_v)
    for step in range(1, STEPS):
        out = send_layers(step, o_h, o_u, o_v)
        substeps()
        wait_layers(out)
        layer_step(step, o_h, o_u, o_v)
    o_eta[...] = X[0, own, 0:ny]
    o_bu[...] = X[1, own, 0:ny]
    o_bv[...] = X[2, own, 0:ny]


def body(zonal_devices, merid_devices, *args):
    height, _, _, thickness = args[:4]
    layers, nx, ny = thickness.shape
    up = -(-layers // 8) * 8
    f32 = jnp.float32
    vmem = pl.BlockSpec(memory_space=pltpu.VMEM)
    smem = pl.BlockSpec(memory_space=pltpu.SMEM)
    extra = FIELDS * (MARGIN - 8)
    plane = jax.ShapeDtypeStruct((nx, ny), f32)
    solid = jax.ShapeDtypeStruct((layers, nx, ny), f32)
    return pl.pallas_call(
        functools.partial(kernel, zonal_devices, merid_devices),
        out_shape=(plane, plane, plane, solid, solid, solid),
        in_specs=[vmem] * 7 + [smem] * 2 + [vmem],
        out_specs=[vmem] * 6,
        scratch_shapes=[
            pltpu.VMEM((FIELDS, 3 * nx, ny + LANES), f32),
            pltpu.VMEM((FIELDS, 3 * nx, LANES), f32),
            pltpu.VMEM((2, 3 * nx, ny + LANES), f32),
            pltpu.VMEM((2, 3 * nx, LANES), f32),
            pltpu.VMEM((2, extra, ny), f32),
            pltpu.VMEM((2, extra, ny), f32),
            pltpu.VMEM((3, nx, LANES), f32),
            pltpu.VMEM((3, nx, LANES), f32),
            pltpu.VMEM((3, nx, LANES), f32),
            pltpu.VMEM((2, nx, ny), f32),
            pltpu.VMEM((2, nx, ny), f32),
            pltpu.VMEM((STEPS, 2 * up, ny), f32),
            pltpu.VMEM((STEPS, up, ny), f32),
            pltpu.VMEM((STEPS, 2 * up, ny), f32),
            pltpu.VMEM((STEPS, up, ny), f32),
            pltpu.VMEM((STEPS, 3, nx, LANES), f32),
            pltpu.VMEM((STEPS, 2, nx, LANES), f32),
            pltpu.SemaphoreType.DMA((10,)),
            pltpu.SemaphoreType.DMA((10,)),
            pltpu.SemaphoreType.DMA((STEPS, 4)),
            pltpu.SemaphoreType.DMA((STEPS, 4)),
        ],
        compiler_params=pltpu.CompilerParams(
            collective_id=0, has_side_effects=True, vmem_limit_bytes=60 * 1024 * 1024
        ),
        name="ocean",
    )(*args)


def solution(mesh):
    field = P(("members", "zonal"), "merid")
    solid = P(None, ("members", "zonal"), "merid")
    fixed = P(None, "zonal", "merid")
    return jax.shard_map(
        functools.partial(body, mesh.shape["zonal"], mesh.shape["merid"]),
        mesh=mesh,
        in_specs=(
            field, field, field, solid, solid, solid, fixed, P("members", None), P("members"), fixed,
        ),
        out_specs=(field, field, field, solid, solid, solid),
        check_vma=False,
    )
```

time: 288 us -> 38.2 us (0.13)
  blocking collectives: 157 us -> 0 us
  other arithmetic: 46 us -> 0 us
  local copies, waits for them, and re-layouts: 52 us -> 7.93 us
  Pallas kernels: 0 us -> 29.3 us
  starting transfers between devices: 27.8 us -> 0 us
    all_gather x5 -> x0, blocking collectives: 157 us -> none  [the longest x2 62.7 us: mirror_state(): whole = lax.all_gather(block, 'zonal', axis=1, tiled=True)]
    pallas_call x0 -> x1, Pallas kernels: none -> 29.3 us  [body(): pl.pallas_call(functools.partial(kernel, zonal_devices, merid_devices), o...]
    ppermute x20 -> x0, starting transfers between devices: 27.8 us -> none  [the longest x10 24.4 us: extended(): after = lax.ppermute(leading, axis, down)]
    slice x78 -> x0, local copies, waits for them, and re-layouts: 24.2 us -> none  [the longest x44 15.4 us: from_high(): lax.slice_in_dim(field, 1, length, axis=axis)]
    mul x28 -> x0, other arithmetic: 16.1 us -> none  [the longest x21 12.1 us: update_flows(): mask_u * (state[1] - wave * (from_high(surface, 0) - surface) + stress_x)]
    another operation x9 -> x0, other arithmetic: 9.38 us -> none  [the longest x2 4.4 us: body(): pressure = jnp.cumsum(thick, axis=0)]
    rev x24 -> x0, local copies, waits for them, and re-layouts: 8.98 us -> none  [the longest x12 6.69 us: wide_substeps(): jnp.flip(far_eta[:, margin - 1], 0)[:, None]]
    div x7 -> x0, other arithmetic: 5.31 us -> none  [the longest x2 2.54 us: body(): (mean_u - jnp.sum(thick_u * trial_u, axis=0)) / depth_u]
  transfers between devices with their start and end apart: 20 -> 0, of which waited for: 6 -> 0; matrix products, arithmetic and copies ran while one was open for 21% -> 0% of each run, Pallas kernels for 0% -> 0%
where the time goes in v1:
time: 38.2 us; the launch traced here: 37.9 us
  Pallas kernels  29.3 us (77%)
  local copies, waits for them, and re-layouts  7.93 us (21%)
  between operations  0.65 us (2%)
    pallas_call x1, Pallas kernels, body(): pl.pallas_call(functools.partial(kernel, zonal_devices, merid_devices), o...  29.3 us
    unnamed x15, local copies, waits for them, and re-layouts  7.93 us

profile of v1, /device:TPU:0, one launch (start us, length us, event | category | flops | bytes accessed | tf_op | source)
XLA Modules:
  0.0 37.9 jit_solution(5610609993576952224)
XLA Ops:
  0.6 1.3 %copy.16.seeds = s32[4,2]{1,0:T(4,128)} copy(s32[4,2]{0,1:T(2,128)} %param.17) | data formatting | bytes 64 | tf_op args[7]
  2.0 29.3 %ocean.1 = (f32[16,512]{1,0:T(8,128)}, f32[16,512]{1,0:T(8,128)}, f32[16,512]{1,0:T(8,128)}, f32[14,16,512]{2,1,0:T(8,128)}, f32[14,16,512]{2,1,0:T(8,128)}, /*index=5*/f32[14,16,512]{2,1,0:T(8,128)}) custom-call(f32[16,512]{1,0:T(8,128)} %height.1, f32[16,512]{1,0:T(8,128)} %trans_u.1, f32[16,512]{1,0:T(8,128)} %trans_v.1, f32[14,16,512]{2,1,0:T(8,128)} %thick.1, ...), custom_call_target="tpu_custom_call" | custom-call | tf_op jit(solution)/shard_map/ocean/pallas_call | solution.py:387
  31.2 0.0 copy-start.3
  31.2 1.4 %copy.23 = f32[16,512]{1,0:T(8,128)} copy(f32[16,512]{1,0:T(8,128)} %get-tuple-element.12) | data formatting | bytes 65536
  32.6 0.0 copy-done.3
  32.6 0.0 copy-start.2
  32.6 0.6 %copy.24 = f32[16,512]{1,0:T(8,128)} copy(f32[16,512]{1,0:T(8,128)S(1)} %copy-done.3) | data formatting | bytes 65536
  33.3 0.2 copy-done.2
  33.4 0.6 %copy.25 = f32[16,512]{1,0:T(8,128)} copy(f32[16,512]{1,0:T(8,128)S(1)} %copy-done.2) | data formatting | bytes 65536
  34.0 0.0 copy-start.1
  34.0 1.9 %copy.26 = f32[14,16,512]{2,1,0:T(8,128)} copy(f32[14,16,512]{2,1,0:T(8,128)} %get-tuple-element.15) | data formatting | bytes 917504
  35.9 0.0 copy-done.1
  35.9 0.0 copy-start
  35.9 0.8 %copy.27 = f32[14,16,512]{2,1,0:T(8,128)} copy(f32[14,16,512]{2,1,0:T(8,128)S(1)} %copy-done.1) | data formatting | bytes 917504
  36.7 0.4 %copy-done = f32[14,16,512]{2,1,0:T(8,128)S(1)} copy-done((f32[14,16,512]{2,1,0:T(8,128)S(1)}, f32[14,16,512]{2,1,0:T(8,128)}, u32[]{:S(2)}) %copy-start) | copy-done | bytes 458776
  37.1 0.8 %copy.28 = f32[14,16,512]{2,1,0:T(8,128)} copy(f32[14,16,512]{2,1,0:T(8,128)S(1)} %copy-done) | data formatting | bytes 917504
Async XLA Ops:
  31.2 1.4 %copy-start.3 = (f32[16,512]{1,0:T(8,128)S(1)}, f32[16,512]{1,0:T(8,128)}, u32[]{:S(2)}) copy-start(f32[16,512]{1,0:T(8,128)} %get-tuple-element.13) | copy-start | bytes 98308
  32.6 0.8 %copy-start.2 = (f32[16,512]{1,0:T(8,128)S(1)}, f32[16,512]{1,0:T(8,128)}, u32[]{:S(2)}) copy-start(f32[16,512]{1,0:T(8,128)} %get-tuple-element.14) | copy-start | bytes 98308
  34.0 1.9 %copy-start.1 = (f32[14,16,512]{2,1,0:T(8,128)S(1)}, f32[14,16,512]{2,1,0:T(8,128)}, u32[]{:S(2)}) copy-start(f32[14,16,512]{2,1,0:T(8,128)} %get-tuple-element.16) | copy-start | bytes 1376260
  35.9 1.2 %copy-start = (f32[14,16,512]{2,1,0:T(8,128)S(1)}, f32[14,16,512]{2,1,0:T(8,128)}, u32[]{:S(2)}) copy-start(f32[14,16,512]{2,1,0:T(8,128)} %get-tuple-element.17) | copy-start | bytes 1376260

commit v2 on v1

v2 whole, which is shorter than its diff:
```python
import functools
import math

import jax
import jax.numpy as jnp
from jax import lax
from jax.experimental import pallas as pl
from jax.experimental.pallas import tpu as pltpu
from jax.sharding import PartitionSpec as P

NSUB = 6
STEPS = 2
MARGIN = NSUB
PAD = 8

WAVE_LIMIT = 0.225
STRESS_SCALE = 0.1
FLUX_STEP = 0.05
PRESS_COEF = 0.05
LANES = 128
VMEM_BYTES = 67043328
SPARE = 1 << 15
FIELDS = 8
SLOT = LANES // FIELDS
WEST = (NSUB - 1, NSUB, NSUB - 1, NSUB - 1, NSUB - 2, NSUB - 1, NSUB - 1, NSUB - 2)
EAST = (NSUB, NSUB, NSUB) + (NSUB - 1,) * 5
MESH = pl.DeviceIdType.MESH


def roll(value, shift, axis):
    return pltpu.roll(value, shift % value.shape[axis], axis)


def iota(shape, axis):
    return lax.broadcasted_iota(jnp.int32, shape, axis)


def turns(seed, index, total):
    part = seed * index * (1.0 / total)
    angle = (2.0 * math.pi) * (part - jnp.floor(part))
    return jnp.cos(angle), jnp.sin(angle)


def tile_up(count):
    return -(-count // 8) * 8


def layer_step(h_ref, u_ref, v_ref, recv_w, recv_e, packs, mean, mask_u, mask_v, depth, o_h, o_u, o_v, top, deep, sent):
    layers, nx, ny = h_ref.shape
    above = recv_w.shape[0] // 2
    row_id = iota((nx, ny), 0)
    lane_id = iota((nx, ny), 1)
    at_west = row_id == 0
    at_east = row_id == nx - 1
    at_south = lane_id == 0
    at_north = lane_id == ny - 1
    zero = jnp.zeros((nx, ny), jnp.float32)
    press_u, press_v, sum_u, sum_v = zero, zero, zero, zero
    deep_u, deep_v = zero, zero
    for l in range(layers):
        h, u, v = h_ref[l], u_ref[l], v_ref[l]
        side = packs[0, :, l : l + 1]
        cap = jnp.where(top, packs[1, :, l : l + 1], side)
        south_v = packs[0, :, layers + l : layers + l + 1]
        h_east = jnp.where(at_east, recv_e[l : l + 1, :], roll(h, -1, 0))
        h_north = jnp.where(at_north, cap, roll(h, -1, 1))
        hu = (h + h_east) * 0.5
        hv = (h + h_north) * 0.5
        if deep:
            deep_u = deep_u + hu
            deep_v = deep_v + hv
        flux_u = u * hu
        flux_v = v * hv
        west_row = recv_w[above + l : above + l + 1, :] * ((recv_w[l : l + 1, :] + h[0:1, :]) * 0.5)
        south_col = jnp.where(top, south_v * ((side + h[:, 0:1]) * 0.5), 0.0)
        flux_w = jnp.where(at_west, west_row, roll(flux_u, 1, 0))
        flux_s = jnp.where(at_south, south_col, roll(flux_v, 1, 1))
        press_u = press_u + (h_east - h)
        press_v = press_v + (h_north - h)
        trial_u = u - PRESS_COEF * press_u
        trial_v = v - PRESS_COEF * press_v
        sum_u = sum_u + hu * trial_u
        sum_v = sum_v + hv * trial_v
        o_u[l] = trial_u
        o_v[l] = trial_v
        o_h[l] = h - FLUX_STEP * (flux_u - flux_w + flux_v - flux_s)
    sent(0)
    if deep:
        depth[0] = 1.0 / deep_u
        depth[1] = 1.0 / deep_v
    fix_u = (mean[0] * (1.0 / NSUB) - sum_u) * depth[0]
    fix_v = (mean[1] * (1.0 / NSUB) - sum_v) * depth[1]
    for l in range(layers):
        o_u[l] = mask_u * (o_u[l] + fix_u)
    sent(1)
    for l in range(layers):
        o_v[l] = mask_v * (o_v[l] + fix_v)
    sent(2)


def last_kernel(
    aux, h_ref, u_ref, v_ref, recv_w, recv_e, packs, o_eta, o_bu, o_bv, o_h, o_u, o_v, n_h, n_u, n_v, sems
):
    top = lax.axis_index("merid") == lax.axis_size("merid") - 1
    flat = [pltpu.make_async_copy(aux.at[k], o, sems.at[3 + k]) for k, o in enumerate((o_eta, o_bu, o_bv))]
    for copy in flat:
        copy.start()
    out = [pltpu.make_async_copy(n, o, sems.at[k]) for k, (n, o) in enumerate(((n_h, o_h), (n_u, o_u), (n_v, o_v)))]
    layer_step(
        h_ref, u_ref, v_ref, recv_w, recv_e, packs, aux.at[3:5], aux[7], aux[8], aux.at[5:7],
        n_h, n_u, n_v, top, False, lambda k: out[k].start(),
    )
    for copy in flat + out:
        copy.wait()


def kernel(
    zonal_devices,
    merid_devices,
    height_any,
    trans_u_any,
    trans_v_any,
    thick_any,
    vel_u_any,
    vel_v_any,
    faces_any,
    seeds_any,
    scale_any,
    base_any,
    aux,
    o_h,
    o_u,
    o_v,
    o_recv_w,
    o_recv_e,
    o_packs,
    thick,
    vel_u,
    vel_v,
    faces,
    seeds,
    scale,
    X,
    G,
    wind_own,
    wind_far,
    west_send,
    west_recv,
    east_send,
    east_recv,
    pack_send,
    inner_recv,
    fold_recv,
    lay_send_r,
    lay_send_l,
    lay_recv_w,
    lay_recv_e,
    lay_pack_send,
    lay_pack_recv,
    load_sem,
    send_sem,
    recv_sem,
    lay_send_sem,
    lay_recv_sem,
):
    layers, nx, ny = thick.shape
    Z = zonal_devices
    total_x, total_y = nx * Z, ny * merid_devices
    z = lax.axis_index("zonal")
    m = lax.axis_index("merid")
    other = 1 - m
    bottom = m == 0
    top = m == merid_devices - 1
    right, left = lax.rem(z + 1, Z), lax.rem(z + Z - 1, Z)
    mirror = Z - 1 - z
    mirror_e, mirror_w = lax.rem(mirror + 1, Z), lax.rem(mirror + Z - 1, Z)
    rows = nx + 2 * PAD
    width = ny + LANES
    last = ny - LANES
    own = slice(PAD, PAD + nx)
    lane = iota((nx, LANES), 1)

    moves = (
        (thick_any, thick),
        (faces_any, faces),
        (height_any, X.at[0, own, 0:ny]),
        (trans_u_any, X.at[1, own, 0:ny]),
        (trans_v_any, X.at[2, own, 0:ny]),
        (base_any, X.at[6:8, own, 0:ny]),
        (vel_u_any, vel_u),
        (vel_v_any, vel_v),
        (seeds_any, seeds),
        (scale_any, scale),
    )
    loads = [pltpu.make_async_copy(src, dst, load_sem.at[k]) for k, (src, dst) in enumerate(moves)]
    for load in loads:
        load.start()

    barrier = pltpu.get_barrier_semaphore()
    for zz, mm in ((left, m), (right, m), (left, other), (right, other), (z, other)):
        pl.semaphore_signal(barrier, inc=1, device_id={"zonal": zz, "merid": mm}, device_id_type=MESH)
    for zz in (mirror_w, mirror, mirror_e):

        @pl.when(jnp.logical_and(top, zz != z))
        def _():
            pl.semaphore_signal(barrier, inc=1, device_id={"zonal": zz}, device_id_type=MESH)

    loads[1].wait()
    X[3, own, 0:ny] = faces[0].astype(jnp.float32)
    X[4, own, 0:ny] = faces[1].astype(jnp.float32)
    loads[0].wait()
    total = thick[0]
    for l in range(1, layers):
        total = total + thick[l]
    X[5, own, 0:ny] = (WAVE_LIMIT / layers) * total

    def pack_tile(step, fields):
        at = 0
        for f in range(fields):
            west_send[step, at : at + WEST[f], :] = X[f, PAD + nx - WEST[f] : PAD + nx, 0:ny]
            at += WEST[f]
        at = 0
        for f in range(fields):
            east_send[step, at : at + EAST[f], :] = X[f, PAD : PAD + EAST[f], 0:ny]
            at += EAST[f]
        inner = jnp.zeros((nx, LANES), jnp.float32)
        crest = jnp.zeros((nx, LANES), jnp.float32)
        for f in range(fields):
            here = jnp.logical_and(lane >= f * SLOT, lane < (f + 1) * SLOT)
            high = roll(X[f, own, last:ny], SLOT * (f + 1), 1)
            low = roll(X[f, own, 0:LANES], SLOT * f, 1)
            crest = jnp.where(here, high, crest)
            inner = jnp.where(here, jnp.where(bottom, high, low), inner)
        pack_send[step, 0] = inner
        pack_send[step, 2] = crest
        for r in range(nx):
            pack_send[step, 1, r : r + 1, :] = pack_send[step, 2, nx - 1 - r : nx - r, :]

    def send_tile(step, fields):
        def send(src, dst, k, zz, mm):
            return pltpu.make_async_remote_copy(
                src_ref=src,
                dst_ref=dst,
                send_sem=send_sem.at[step, k],
                recv_sem=recv_sem.at[step, k],
                device_id={"zonal": zz, "merid": mm},
                device_id_type=MESH,
            )

        west, east = tile_up(sum(WEST[:fields])), tile_up(sum(EAST[:fields]))
        tail, whole, start = slice(nx - PAD, nx), slice(0, nx), slice(0, PAD)
        places = (slice(0, PAD), own, slice(PAD + nx, rows))
        inner = lambda s, part: (pack_send.at[step, 0, part], inner_recv.at[step, places[s]])
        copies = [
            send(*inner(2, start), 4, left, other),
            send(*inner(1, whole), 5, z, other),
            send(*inner(0, tail), 6, right, other),
            send(west_send.at[step, 0:west], west_recv.at[step, 0:west], 0, right, m),
            send(east_send.at[step, 0:east], east_recv.at[step, 0:east], 1, left, m),
        ]
        folds = []
        for s, part, zz in ((2, start, mirror_w), (1, whole, mirror), (0, tail, mirror_e)):
            src, dst = pack_send.at[step, 1, part], fold_recv.at[step, places[s]]
            near = pltpu.make_async_copy(src, dst, recv_sem.at[step, 7 + s])
            folds.append((send(src, dst, 7 + s, zz, m), near, zz))
        for far_copy, near_copy, zz in folds:

            @pl.when(jnp.logical_and(top, zz != z))
            def _():
                far_copy.start()

            @pl.when(jnp.logical_and(top, zz == z))
            def _():
                near_copy.start()

        for copy in copies:
            copy.start()
        return copies, folds

    def take_tile(step, fields, copies, folds):
        for copy in copies:
            copy.wait()
        for far_copy, near_copy, zz in folds:

            @pl.when(jnp.logical_and(top, zz != z))
            def _():
                far_copy.wait()

            @pl.when(jnp.logical_and(top, zz == z))
            def _():
                near_copy.wait()

        at = 0
        for f in range(fields):
            X[f, PAD - WEST[f] : PAD, 0:ny] = west_recv[step, at : at + WEST[f], :]
            at += WEST[f]
        at = 0
        for f in range(fields):
            X[f, PAD + nx : PAD + nx + EAST[f], 0:ny] = east_recv[step, at : at + EAST[f], :]
            at += EAST[f]
        for f in range(fields):
            got = inner_recv[step]
            X[f, :, ny:width] = jnp.where(
                top, roll(got, LANES - SLOT * (f + 1), 1), roll(got, LANES - SLOT * f, 1)
            )
            G[f] = roll(fold_recv[step], LANES - SLOT * (f + 1), 1)

    for load in loads[2:6]:
        load.wait()
    pack_tile(0, FIELDS)
    across = sum((zz != z).astype(jnp.int32) for zz in (mirror_w, mirror, mirror_e))
    pl.semaphore_wait(barrier, 5 + jnp.where(top, across, 0))
    tile = send_tile(0, FIELDS)

    def lay_copies(step):
        def one(src, dst, k, zz, mm):
            return pltpu.make_async_remote_copy(
                src_ref=src,
                dst_ref=dst,
                send_sem=lay_send_sem.at[step, k],
                recv_sem=lay_recv_sem.at[step, k],
                device_id={"zonal": zz, "merid": mm},
                device_id_type=MESH,
            )

        return [
            one(lay_send_r.at[step], lay_recv_w.at[step], 0, right, m),
            one(lay_send_l.at[step], lay_recv_e.at[step], 1, left, m),
            one(lay_pack_send.at[step, 0], lay_pack_recv.at[step, 0], 2, z, other),
            one(lay_pack_send.at[step, 1], lay_pack_recv.at[step, 1], 3, mirror, m),
        ]

    above = lay_send_r.shape[1] // 2

    def send_layers(step, h_ref, u_ref, v_ref):
        edge = jnp.zeros((nx, LANES), jnp.float32)
        brim = jnp.zeros((nx, LANES), jnp.float32)
        for l in range(layers):
            lay_send_r[step, l : l + 1, :] = h_ref[l, nx - 1 : nx, :]
            lay_send_r[step, above + l : above + l + 1, :] = u_ref[l, nx - 1 : nx, :]
            lay_send_l[step, l : l + 1, :] = h_ref[l, 0:1, :]
            high = roll(h_ref[l, :, last:ny], l + 1, 1)
            low = roll(h_ref[l, :, 0:LANES], l, 1)
            high_v = roll(v_ref[l, :, last:ny], layers + l + 1, 1)
            edge = jnp.where(lane == l, jnp.where(bottom, high, low), edge)
            edge = jnp.where(lane == layers + l, high_v, edge)
            brim = jnp.where(lane == l, high, brim)
        lay_pack_send[step, 0] = edge
        lay_pack_send[step, 2] = brim
        for r in range(nx):
            lay_pack_send[step, 1, r : r + 1, :] = lay_pack_send[step, 2, nx - 1 - r : nx - r, :]
        out = lay_copies(step)
        for copy in out[:3]:
            copy.start()

        @pl.when(top)
        def _():
            out[3].start()

        return out

    def wait_layers(out):
        for copy in out[:3]:
            copy.wait()

        @pl.when(top)
        def _():
            out[3].wait()

    for load in loads[6:]:
        load.wait()
    out = send_layers(0, thick, vel_u, vel_v)

    first = (z * nx - PAD).astype(jnp.float32)
    col = first + iota((rows, 1), 0).astype(jnp.float32) + float(total_x)
    far_col = float(2 * total_x - 1) - (first + iota((rows, 1), 0).astype(jnp.float32))
    spot = iota((1, width), 1)
    row = spot + m * ny
    row = jnp.where(jnp.logical_and(top, spot >= ny), row - width, row).astype(jnp.float32)
    far_row = (iota((1, LANES), 1) + (total_y - LANES)).astype(jnp.float32)
    px = jnp.zeros((rows, width), jnp.float32)
    py = jnp.zeros((rows, width), jnp.float32)
    fx = jnp.zeros((rows, LANES), jnp.float32)
    fy = jnp.zeros((rows, LANES), jnp.float32)
    for k in range(seeds.shape[1]):
        seed_x = seeds[0, k].astype(jnp.float32)
        seed_y = seeds[1, k].astype(jnp.float32)
        ca, sa = turns(seed_x, col, total_x)
        cf, sf = turns(seed_x, far_col, total_x)
        cb, sb = turns(seed_y, row, total_y)
        cg, sg = turns(seed_y, far_row, total_y)
        amp = scale[k]
        ca, sa, cf, sf = amp * ca, amp * sa, amp * cf, amp * sf
        px = px + (ca * cb - sa * sb)
        py = py + (sa * cb + ca * sb)
        fx = fx + (cf * cg - sf * sg)
        fy = fy + (sf * cg + cf * sg)
    wind_own[0] = px
    wind_own[1] = py
    wind_far[0] = fx
    wind_far[1] = fy

    take_tile(0, FIELDS, *tile)
    for k in range(2):
        X[6 + k] = STRESS_SCALE * (X[6 + k] + wind_own[k])
        G[6 + k] = STRESS_SCALE * (G[6 + k] + wind_far[k])

    lanes = iota((rows, width), 1)
    wall = jnp.logical_and(bottom, lanes == 0)
    crown = jnp.logical_and(top, lanes == ny - 1)
    far_top = iota((rows, LANES), 1) == LANES - 1

    def substep(_, carry):
        eta, bu, bv = X[0], X[1], X[2]
        g_eta, g_bu, g_bv = G[0], G[1], G[2]
        eta = eta - (bu - roll(bu, 1, 0) + bv - jnp.where(wall, 0.0, roll(bv, 1, 1)))
        g_eta = g_eta - (g_bu - roll(g_bu, -1, 0) + g_bv - roll(g_bv, 1, 1))
        north = jnp.where(crown, g_eta[:, LANES - 1 :], roll(eta, -1, 1))
        g_north = jnp.where(far_top, eta[:, ny - 1 : ny], roll(g_eta, -1, 1))
        bu = X[3] * (bu - X[5] * (roll(eta, -1, 0) - eta) + X[6])
        bv = X[4] * (bv - X[5] * (north - eta) + X[7])
        g_bu = G[3] * (g_bu - G[5] * (roll(g_eta, 1, 0) - g_eta) + G[6])
        g_bv = G[4] * (g_bv - G[5] * (g_north - g_eta) + G[7])
        X[0], X[1], X[2] = eta, bu, bv
        G[0], G[1], G[2] = g_eta, g_bu, g_bv
        aux[3] = aux[3] + bu[own, 0:ny]
        aux[4] = aux[4] + bv[own, 0:ny]
        return carry

    def substeps():
        aux[3:5] = jnp.zeros((2, nx, ny), jnp.float32)
        lax.fori_loop(0, NSUB, substep, 0)

    aux[7] = X[3, own, 0:ny]
    aux[8] = X[4, own, 0:ny]
    h_ref, u_ref, v_ref = thick, vel_u, vel_v
    for step in range(STEPS - 1):
        substeps()
        pack_tile(step + 1, 3)
        tile = send_tile(step + 1, 3)
        wait_layers(out)
        layer_step(
            h_ref, u_ref, v_ref, lay_recv_w.at[step], lay_recv_e.at[step], lay_pack_recv.at[step],
            aux.at[3:5], aux[7], aux[8], aux.at[5:7], o_h, o_u, o_v, top, step == 0, lambda k: None,
        )
        h_ref, u_ref, v_ref = o_h, o_u, o_v
        out = send_layers(step + 1, o_h, o_u, o_v)
        take_tile(step + 1, 3, *tile)
    substeps()
    for f in range(3):
        aux[f] = X[f, own, 0:ny]
    wait_layers(out)
    o_recv_w[...] = lay_recv_w[STEPS - 1]
    o_recv_e[...] = lay_recv_e[STEPS - 1]
    o_packs[...] = lay_pack_recv[STEPS - 1]


def body(zonal_devices, merid_devices, *args):
    thickness = args[3]
    layers, nx, ny = thickness.shape
    up = tile_up(layers)
    f32 = jnp.float32
    vmem = pl.BlockSpec(memory_space=pltpu.VMEM)
    far = pl.BlockSpec(memory_space=pltpu.HBM)
    hbm = pl.BlockSpec(memory_space=pl.ANY)
    rows = nx + 2 * PAD
    west, east = tile_up(sum(WEST)), tile_up(sum(EAST))
    plane = jax.ShapeDtypeStruct((nx, ny), f32)
    solid = jax.ShapeDtypeStruct((layers, nx, ny), f32)
    kept = [
        (9, nx, ny), (layers, nx, ny), (layers, nx, ny), (layers, nx, ny), (2 * up, ny), (up, ny), (2, nx, LANES),
    ]
    room = sum(math.prod(shape) for shape in kept)
    args = list(args)
    args[7] = args[7].T
    between = pl.pallas_call(
        functools.partial(kernel, zonal_devices, merid_devices),
        out_shape=[pltpu.VMEM(shape, f32) for shape in kept],
        in_specs=[far] * 10,
        out_specs=[vmem] * len(kept),
        scratch_shapes=[
            pltpu.VMEM((layers, nx, ny), f32),
            pltpu.VMEM((layers, nx, ny), f32),
            pltpu.VMEM((layers, nx, ny), f32),
            pltpu.VMEM((2, nx, ny), jnp.int32),
            pltpu.SMEM(args[7].shape, jnp.int32),
            pltpu.SMEM(args[8].shape, f32),
            pltpu.VMEM((FIELDS, rows, ny + LANES), f32),
            pltpu.VMEM((FIELDS, rows, LANES), f32),
            pltpu.VMEM((2, rows, ny + LANES), f32),
            pltpu.VMEM((2, rows, LANES), f32),
            pltpu.VMEM((STEPS, west, ny), f32),
            pltpu.VMEM((STEPS, west, ny), f32),
            pltpu.VMEM((STEPS, east, ny), f32),
            pltpu.VMEM((STEPS, east, ny), f32),
            pltpu.VMEM((STEPS, 3, nx, LANES), f32),
            pltpu.VMEM((STEPS, rows, LANES), f32),
            pltpu.VMEM((STEPS, rows, LANES), f32),
            pltpu.VMEM((STEPS, 2 * up, ny), f32),
            pltpu.VMEM((STEPS, up, ny), f32),
            pltpu.VMEM((STEPS, 2 * up, ny), f32),
            pltpu.VMEM((STEPS, up, ny), f32),
            pltpu.VMEM((STEPS, 3, nx, LANES), f32),
            pltpu.VMEM((STEPS, 2, nx, LANES), f32),
            pltpu.SemaphoreType.DMA((10,)),
            pltpu.SemaphoreType.DMA((STEPS, 10)),
            pltpu.SemaphoreType.DMA((STEPS, 10)),
            pltpu.SemaphoreType.DMA((STEPS, 4)),
            pltpu.SemaphoreType.DMA((STEPS, 4)),
        ],
        compiler_params=pltpu.CompilerParams(
            collective_id=0, has_side_effects=True, vmem_limit_bytes=VMEM_BYTES - 4 * room - SPARE
        ),
        name="ocean",
    )(*args)
    return pl.pallas_call(
        last_kernel,
        out_shape=(plane, plane, plane, solid, solid, solid),
        in_specs=[vmem] * len(kept),
        out_specs=[hbm] * 6,
        scratch_shapes=[
            pltpu.VMEM((layers, nx, ny), f32),
            pltpu.VMEM((layers, nx, ny), f32),
            pltpu.VMEM((layers, nx, ny), f32),
            pltpu.SemaphoreType.DMA((6,)),
        ],
        compiler_params=pltpu.CompilerParams(vmem_limit_bytes=24 * 1024 * 1024),
        name="last",
    )(*between)


def solution(mesh):
    field = P(("members", "zonal"), "merid")
    solid = P(None, ("members", "zonal"), "merid")
    fixed = P(None, "zonal", "merid")
    return jax.shard_map(
        functools.partial(body, mesh.shape["zonal"], mesh.shape["merid"]),
        mesh=mesh,
        in_specs=(
            field, field, field, solid, solid, solid, fixed, P("members", None), P("members"), fixed,
        ),
        out_specs=(field, field, field, solid, solid, solid),
        check_vma=False,
    )
```

time: 38.2 us -> 24.4 us (0.64)
  local copies, waits for them, and re-layouts: 7.93 us -> 0 us
  Pallas kernels: 29.3 us -> 23.6 us
    pallas_call x1, Pallas kernels: 29.3 us -> 20.9 us  [body(): pl.pallas_call(functools.partial(kernel, zonal_devices, merid_devices), o...]
    unnamed x15 -> x0, local copies, waits for them, and re-layouts: 7.93 us -> none
    pallas_call x0 -> x1, Pallas kernels: none -> 2.71 us  [body(): pl.pallas_call(last_kernel, out_shape=(plane, plane, plane, solid, solid,...]
where the time goes in v2:
time: 24.4 us; the launch traced here: 24.2 us
  Pallas kernels  23.6 us (97%)
  between operations  0.64 us (3%)
    pallas_call x1, Pallas kernels, body(): pl.pallas_call(functools.partial(kernel, zonal_devices, merid_devices), o...  20.9 us
    pallas_call x1, Pallas kernels, body(): pl.pallas_call(last_kernel, out_shape=(plane, plane, plane, solid, solid,...  2.71 us

profile of v2, /device:TPU:0, one launch (start us, length us, event | category | flops | bytes accessed | tf_op | source)
XLA Modules:
  0.0 24.2 jit_solution(13865835629668444522)
XLA Ops:
  0.6 20.9 %ocean.1 = (f32[9,16,512]{2,1,0:T(8,128)S(1)}, f32[14,16,512]{2,1,0:T(8,128)S(1)}, f32[14,16,512]{2,1,0:T(8,128)S(1)}, f32[14,16,512]{2,1,0:T(8,128)S(1)}, f32[3...) custom-call(f32[16,512]{1,0:T(8,128)} %height_any.1, f32[16,512]{1,0:T(8,128)} %trans_u_any.1, ...), custom_call_target="tpu_custom_call" | custom-call | tf_op jit(solution)/shard_map/ocean/pallas_call | solution.py:476
  21.5 2.7 %last.1 = (f32[16,512]{1,0:T(8,128)}, f32[16,512]{1,0:T(8,128)}, f32[16,512]{1,0:T(8,128)}, f32[14,16,512]{2,1,0:T(8,128)}, f32[14,16,512]{2,1,0:T(8,128)}, /*index=5*/f32[14,16,512]{2,1,0:T(8,128)}) custom-call(f32[9,16,512]{2,1,0:T(8,128)S(1)} %get-tuple-element.13.aux, f32[14,16,512]{2,1,0:T(8,128)S(1)} %get-tuple-element.14.h_ref, ...), custom_call_target="tpu_custom_call" | custom-call | tf_op jit(solution)/shard_map/last/pallas_call | solution.py:516

commit v3 on v2

--- a/solution.py
+++ b/solution.py
@@ -24,6 +24,8 @@
 SLOT = LANES // FIELDS
 WEST = (NSUB - 1, NSUB, NSUB - 1, NSUB - 1, NSUB - 2, NSUB - 1, NSUB - 1, NSUB - 2)
 EAST = (NSUB, NSUB, NSUB) + (NSUB - 1,) * 5
+ORDER = (0, 1, 2, 3, 4, 6, 7, 5)
+CUT = 32
 MESH = pl.DeviceIdType.MESH
 
 
@@ -180,13 +182,22 @@
     own = slice(PAD, PAD + nx)
     lane = iota((nx, LANES), 1)
 
+    barrier = pltpu.get_barrier_semaphore()
+    for zz, mm in ((left, m), (right, m), (left, other), (right, other), (z, other)):
+        pl.semaphore_signal(barrier, inc=1, device_id={"zonal": zz, "merid": mm}, device_id_type=MESH)
+    for zz in (mirror_w, mirror, mirror_e):
+
+        @pl.when(jnp.logical_and(top, zz != z))
+        def _():
+            pl.semaphore_signal(barrier, inc=1, device_id={"zonal": zz}, device_id_type=MESH)
+
     moves = (
-        (thick_any, thick),
         (faces_any, faces),
         (height_any, X.at[0, own, 0:ny]),
         (trans_u_any, X.at[1, own, 0:ny]),
         (trans_v_any, X.at[2, own, 0:ny]),
         (base_any, X.at[6:8, own, 0:ny]),
+        (thick_any, thick),
         (vel_u_any, vel_u),
         (vel_v_any, vel_v),
         (seeds_any, seeds),
@@ -196,33 +207,22 @@
     for load in loads:
         load.start()
 
-    barrier = pltpu.get_barrier_semaphore()
-    for zz, mm in ((left, m), (right, m), (left, other), (right, other), (z, other)):
-        pl.semaphore_signal(barrier, inc=1, device_id={"zonal": zz, "merid": mm}, device_id_type=MESH)
-    for zz in (mirror_w, mirror, mirror_e):
-
-        @pl.when(jnp.logical_and(top, zz != z))
-        def _():
-            pl.semaphore_signal(barrier, inc=1, device_id={"zonal": zz}, device_id_type=MESH)
-
-    loads[1].wait()
+    loads[0].wait()
     X[3, own, 0:ny] = faces[0].astype(jnp.float32)
     X[4, own, 0:ny] = faces[1].astype(jnp.float32)
-    loads[0].wait()
-    total = thick[0]
-    for l in range(1, layers):
-        total = total + thick[l]
-    X[5, own, 0:ny] = (WAVE_LIMIT / layers) * total
-
-    def pack_tile(step, fields):
-        at = 0
-        for f in range(fields):
-            west_send[step, at : at + WEST[f], :] = X[f, PAD + nx - WEST[f] : PAD + nx, 0:ny]
-            at += WEST[f]
-        at = 0
-        for f in range(fields):
-            east_send[step, at : at + EAST[f], :] = X[f, PAD : PAD + EAST[f], 0:ny]
-            at += EAST[f]
+    for load in loads[1:5]:
+        load.wait()
+
+    def pack_rows(step, start, stop):
+        west = sum(WEST[f] for f in ORDER[:start])
+        east = sum(EAST[f] for f in ORDER[:start])
+        for f in ORDER[start:stop]:
+            west_send[step, west : west + WEST[f], :] = X[f, PAD + nx - WEST[f] : PAD + nx, 0:ny]
+            east_send[step, east : east + EAST[f], :] = X[f, PAD : PAD + EAST[f], 0:ny]
+            west += WEST[f]
+            east += EAST[f]
+
+    def pack_edges(step, fields):
         inner = jnp.zeros((nx, LANES), jnp.float32)
         crest = jnp.zeros((nx, LANES), jnp.float32)
         for f in range(fields):
@@ -247,7 +247,15 @@
                 device_id_type=MESH,
             )
 
-        west, east = tile_up(sum(WEST[:fields])), tile_up(sum(EAST[:fields]))
+        bulk = []
+        for src, dst, k, zz, count in (
+            (west_send, west_recv, 0, right, tile_up(sum(WEST[:fields]))),
+            (east_send, east_recv, 1, left, tile_up(sum(EAST[:fields]))),
+        ):
+            cuts = [0, CUT, count] if count > CUT else [0, count]
+            for n, (low, high) in enumerate(zip(cuts[:-1], cuts[1:])):
+                part = slice(low, high)
+                bulk.append((n, send(src.at[step, part], dst.at[step, part], k + 2 * n, zz, m)))
         tail, whole, start = slice(nx - PAD, nx), slice(0, nx), slice(0, PAD)
         places = (slice(0, PAD), own, slice(PAD + nx, rows))
         inner = lambda s, part: (pack_send.at[step, 0, part], inner_recv.at[step, places[s]])
@@ -255,14 +263,15 @@
             send(*inner(2, start), 4, left, other),
             send(*inner(1, whole), 5, z, other),
             send(*inner(0, tail), 6, right, other),
-            send(west_send.at[step, 0:west], west_recv.at[step, 0:west], 0, right, m),
-            send(east_send.at[step, 0:east], east_recv.at[step, 0:east], 1, left, m),
         ]
         folds = []
         for s, part, zz in ((2, start, mirror_w), (1, whole, mirror), (0, tail, mirror_e)):
             src, dst = pack_send.at[step, 1, part], fold_recv.at[step, places[s]]
             near = pltpu.make_async_copy(src, dst, recv_sem.at[step, 7 + s])
             folds.append((send(src, dst, 7 + s, zz, m), near, zz))
+        return [c for n, c in bulk if n == 0], [c for n, c in bulk if n > 0] + copies, folds
+
+    def start_rest(copies, folds):
         for far_copy, near_copy, zz in folds:
 
             @pl.when(jnp.logical_and(top, zz != z))
@@ -275,10 +284,9 @@
 
         for copy in copies:
             copy.start()
-        return copies, folds
-
-    def take_tile(step, fields, copies, folds):
-        for copy in copies:
+
+    def take_tile(step, fields, bulk, copies, folds):
+        for copy in bulk + copies:
             copy.wait()
         for far_copy, near_copy, zz in folds:
 
@@ -290,14 +298,12 @@
             def _():
                 near_copy.wait()
 
-        at = 0
-        for f in range(fields):
-            X[f, PAD - WEST[f] : PAD, 0:ny] = west_recv[step, at : at + WEST[f], :]
-            at += WEST[f]
-        at = 0
-        for f in range(fields):
-            X[f, PAD + nx : PAD + nx + EAST[f], 0:ny] = east_recv[step, at : at + EAST[f], :]
-            at += EAST[f]
+        west = east = 0
+        for f in ORDER[:fields]:
+            X[f, PAD - WEST[f] : PAD, 0:ny] = west_recv[step, west : west + WEST[f], :]
+            X[f, PAD + nx : PAD + nx + EAST[f], 0:ny] = east_recv[step, east : east + EAST[f], :]
+            west += WEST[f]
+            east += EAST[f]
         for f in range(fields):
             got = inner_recv[step]
             X[f, :, ny:width] = jnp.where(
@@ -305,12 +311,23 @@
             )
             G[f] = roll(fold_recv[step], LANES - SLOT * (f + 1), 1)
 
-    for load in loads[2:6]:
-        load.wait()
-    pack_tile(0, FIELDS)
+    def post_bulk(tile):
+        for copy in tile[0]:
+            copy.start()
+
+    pack_rows(0, 0, FIELDS - 1)
     across = sum((zz != z).astype(jnp.int32) for zz in (mirror_w, mirror, mirror_e))
     pl.semaphore_wait(barrier, 5 + jnp.where(top, across, 0))
     tile = send_tile(0, FIELDS)
+    post_bulk(tile)
+    loads[5].wait()
+    total = thick[0]
+    for l in range(1, layers):
+        total = total + thick[l]
+    X[5, own, 0:ny] = (WAVE_LIMIT / layers) * total
+    pack_rows(0, FIELDS - 1, FIELDS)
+    pack_edges(0, FIELDS)
+    start_rest(*tile[1:])
 
     def lay_copies(step):
         def one(src, dst, k, zz, mm):
@@ -429,15 +446,18 @@
 
     def substeps():
         aux[3:5] = jnp.zeros((2, nx, ny), jnp.float32)
-        lax.fori_loop(0, NSUB, substep, 0)
+        lax.fori_loop(0, NSUB, substep, 0, unroll=True)
 
     aux[7] = X[3, own, 0:ny]
     aux[8] = X[4, own, 0:ny]
     h_ref, u_ref, v_ref = thick, vel_u, vel_v
     for step in range(STEPS - 1):
         substeps()
-        pack_tile(step + 1, 3)
+        pack_rows(step + 1, 0, 3)
         tile = send_tile(step + 1, 3)
+        post_bulk(tile)
+        pack_edges(step + 1, 3)
+        start_rest(*tile[1:])
         wait_layers(out)
         layer_step(
             h_ref, u_ref, v_ref, lay_recv_w.at[step], lay_recv_e.at[step], lay_pack_recv.at[step],

time: 24.4 us -> 24.2 us (level)
  no operation moved by 1% of the time
where the time goes in v3:
time: 24.2 us; the launch traced here: 24.1 us
  Pallas kernels  23.4 us (97%)
  between operations  0.64 us (3%)
    pallas_call x1, Pallas kernels, body(): pl.pallas_call(functools.partial(kernel, zonal_devices, merid_devices), o...  20.7 us
    pallas_call x1, Pallas kernels, body(): pl.pallas_call(last_kernel, out_shape=(plane, plane, plane, solid, solid,...  2.71 us

profile of v3, /device:TPU:0, one launch (start us, length us, event | category | flops | bytes accessed | tf_op | source)
XLA Modules:
  0.0 24.1 jit_solution(12098578064024193473)
XLA Ops:
  0.6 20.7 %ocean.1 = (f32[9,16,512]{2,1,0:T(8,128)S(1)}, f32[14,16,512]{2,1,0:T(8,128)S(1)}, f32[14,16,512]{2,1,0:T(8,128)S(1)}, f32[14,16,512]{2,1,0:T(8,128)S(1)}, f32[3...) custom-call(f32[16,512]{1,0:T(8,128)} %height_any.1, f32[16,512]{1,0:T(8,128)} %trans_u_any.1, ...), custom_call_target="tpu_custom_call" | custom-call | tf_op jit(solution)/shard_map/ocean/pallas_call | solution.py:496
  21.3 2.7 %last.1 = (f32[16,512]{1,0:T(8,128)}, f32[16,512]{1,0:T(8,128)}, f32[16,512]{1,0:T(8,128)}, f32[14,16,512]{2,1,0:T(8,128)}, f32[14,16,512]{2,1,0:T(8,128)}, /*index=5*/f32[14,16,512]{2,1,0:T(8,128)}) custom-call(f32[9,16,512]{2,1,0:T(8,128)S(1)} %get-tuple-element.13.aux, f32[14,16,512]{2,1,0:T(8,128)S(1)} %get-tuple-element.14.h_ref, ...), custom_call_target="tpu_custom_call" | custom-call | tf_op jit(solution)/shard_map/last/pallas_call | solution.py:536
